TPU v7x, 8 devices: a whole 2x2x1 slice. The times are simulated.
8 devices in a mesh: dp: 2 (over y, z), tp: 4 (over x, core).
Axes of the slice: x: 2, y: 2, z: 1, core: 2. Of those that a mesh axis runs over, the one named last changes fastest.
Arguments:
- x: bfloat16 [128, 3072], P('dp'), parts along dimension 0
- k_cache: bfloat16 [128, 4096, 8, 128], P('dp', None, 'tp'), parts along dimension 0
- v_cache: bfloat16 [128, 4096, 8, 128], P('dp', None, 'tp'), parts along dimension 0
- gain_a: bfloat16 [3072], replicated
- wq: bfloat16 [3072, 3072], P(None, 'tp')
- wo: bfloat16 [3072, 3072], P('tp')
- gain_m: bfloat16 [3072], replicated
- w_gate: bfloat16 [3072, 8192], P(None, 'tp')
- w_up: bfloat16 [3072, 8192], P(None, 'tp')
- w_down: bfloat16 [8192, 3072], P('tp')
Outputs:
- output: bfloat16 [128, 3072], P('dp'), parts along dimension 0
There are 2 independent parts. A program takes and returns all parts, laid end to end along the dimension named above; an argument that names none is the same for every part.
All inputs are finite; a program needn't handle non-finite values.
Results may differ from a plain program's by a relative error of at most 0.017.
Values are sent between devices in bfloat16 or wider.
A program may use at most 2 GiB of HBM per device.

v0:
```python
import jax
import jax.numpy as jnp
from jax import lax
from jax.sharding import PartitionSpec as P

HEAD = 128
THETA = 10000


def normed(x, gain):
    wide = x.astype(jnp.float32)
    scale = lax.rsqrt(jnp.mean(wide * wide, -1, keepdims=True) + 1e-6)
    return (wide * scale * gain.astype(jnp.float32)).astype(jnp.bfloat16)


def turned(t, place, theta):
    half = t.shape[-1] // 2
    angle = place.astype(jnp.float32)[:, None] * theta ** (-jnp.arange(half, dtype=jnp.float32) / half)
    cos, sin = jnp.cos(angle)[:, None], jnp.sin(angle)[:, None]
    a, b = t[..., :half].astype(jnp.float32), t[..., half:].astype(jnp.float32)
    return jnp.concatenate([a * cos - b * sin, b * cos + a * sin], -1).astype(jnp.bfloat16)


def matmul(a, w):
    return jnp.dot(a, w, preferred_element_type=jnp.float32).astype(jnp.bfloat16)


def einsum(form, a, b):
    return jnp.einsum(form, a.astype(jnp.float32), b.astype(jnp.float32))


def seen_by(a, wq, k_cache, v_cache, head, theta):
    batch, cache, kv_heads = k_cache.shape[:3]
    place = jnp.full((batch,), cache - 1)
    q = turned(matmul(a, wq).reshape(batch, -1, head), place, theta).reshape(batch, kv_heads, -1, head)
    scores = einsum("bgsd,bugd->bgsu", q, k_cache) * head**-0.5
    weights = jax.nn.softmax(scores, -1).astype(jnp.bfloat16)
    return einsum("bgsu,bugd->bgsd", weights, v_cache).astype(jnp.bfloat16).reshape(batch, -1)


def hidden_of(b, w_gate, w_up):
    gate = jnp.dot(b, w_gate, preferred_element_type=jnp.float32)
    up = jnp.dot(b, w_up, preferred_element_type=jnp.float32)
    return (jax.nn.silu(gate) * up).astype(jnp.bfloat16)


def solution(mesh):
    def added(t, term):
        return (t.astype(jnp.float32) + lax.psum(term.astype(jnp.bfloat16), "tp").astype(jnp.float32)).astype(jnp.bfloat16)

    def step(x, k_cache, v_cache, gain_a, wq, wo, gain_m, w_gate, w_up, w_down):
        seen = seen_by(normed(x, gain_a), wq, k_cache, v_cache, HEAD, THETA)
        h = added(x, jnp.dot(seen, wo, preferred_element_type=jnp.float32))
        return added(h, jnp.dot(hidden_of(normed(h, gain_m), w_gate, w_up), w_down, preferred_element_type=jnp.float32))

    states, cache, columns, rows_of = P("dp", None), P("dp", None, "tp", None), P(None, "tp"), P("tp", None)
    return jax.shard_map(
        step,
        mesh=mesh,
        in_specs=(states, cache, cache, P(None), columns, rows_of, P(None), columns, columns, rows_of),
        out_specs=states,
        check_vma=False,
    )
```

profile of v0, /device:TPU:0, one launch (start us, length us, event | category | flops | bytes accessed | tf_op | source)
XLA Modules:
  0.0 227.7 jit_solution(6953578585612729943)
XLA Ops:
  6.5 0.0 all-reduce.3.cloned.1.call-start
  6.6 0.7 convert_element_type.63
  7.3 1.2 fusion.12
  8.5 3.5 %convolution_convert_fusion.2 = bf16[64,768]{1,0:T(8,128)(2,1)S(1)} fusion(bf16[3072,768]{1,0:T(8,128)(2,1)} %param.14, bf16[64,3072]{1,0:T(8,128)(2,1)} %param.10, f32[3072]{0:T(1024)S(1)} %convert_element_type.63, f32[64]{0:T(128)S(1)} %add_rsqrt_fusion.1), kind=kOutput, calls=%fused_computation.22 | convolution fusion | flops 302825472 | bytes 5222656 | tf_op jit(solution)/shard_map/dot_general | solution.py:25
  11.9 0.1 reshape.39
  12.1 0.1 fusion.46
  12.2 0.1 fusion.30
  12.3 0.1 copy.21
  12.4 0.1 copy.22
  12.5 62.3 %fusion.3 = f32[64,2,3,4096]{3,2,1,0:T(4,128)} fusion(bf16[64,4096,2,128]{3,2,1,0:T(2,128)(2,1)} %param.11, bf16[64,2,3,64]{3,2,1,0:T(4,128)(2,1)S(1)} %copy.22, bf16[64,2,3,64]{3,2,1,0:T(4,128)(2,1)S(1)} %copy.21), kind=kOutput, calls=%fused_computation.3 | convolution fusion | flops 402849792 | bytes 140607488 | tf_op jit(solution)/shard_map/bgsd,bugd->bgsu/dot_general | solution.py:29
  74.7 12.9 %fusion.47 = (f32[64,2,3]{2,1,0:T(2,128)S(1)}, f32[64,2,3,4096]{3,2,1,0:T(4,128)}) fusion(f32[64,2,3,4096]{3,2,1,0:T(4,128)} %fusion.3), kind=kOutput, calls=%fused_computation.60 | output fusion | flops 4722687 | bytes 12584448 | tf_op jit(solution)/shard_map/sub | solution.py:37
  87.6 0.0 copy-start.1
  87.6 0.0 copy-start
  87.7 48.3 %fusion.9 = bf16[64,2,3,128]{3,2,1,0:T(4,128)(2,1)S(1)} fusion(bf16[64,4096,2,128]{3,2,1,0:T(2,128)(2,1)} %param.12, f32[64,2,3,4096]{3,2,1,0:T(4,128)} %get-tuple-element.12, f32[64,2,3]{2,1,0:T(2,128)S(1)} %get-tuple-element.11), kind=kOutput, calls=%fused_computation.21 | convolution fusion | flops 405848064 | bytes 140609024 | tf_op jit(solution)/shard_map/bgsu,bugd->bgsd/dot_general | solution.py:29
  136.0 0.1 reshape.40
  136.1 4.0 %convolution_convert_fusion = bf16[64,3072]{1,0:T(8,128)(2,1)} fusion(bf16[64,768]{1,0:T(8,128)(2,1)S(1)} %reshape.40, bf16[768,3072]{1,0:T(8,128)(2,1)} %param.15), kind=kOutput, calls=%fused_computation.11 | convolution fusion | flops 302186496 | bytes 5210112 | tf_op jit(solution)/shard_map/dot_general | solution.py:53
  140.1 0.0 all-reduce.3.cloned.1.call-update
  140.1 0.0 all-reduce.5.cloned.1.call-start
  140.1 0.0 copy-done.1
  140.2 30.0 %all-reduce.3.cloned.1.call-done = bf16[64,3072]{1,0:T(8,128)(2,1)} async-done(((bf16[64,3072]{1,0:T(8,128)(2,1)}), bf16[64,3072]{1,0:T(8,128)(2,1)}) %all-reduce.3.cloned.1.call-update) | async-done | bytes 393232 | tf_op jit(solution)/shard_map/psum | solution.py:49
  170.2 0.0 copy-done
  170.2 1.2 fusion.16
  171.4 6.9 %fusion.38 = f32[64,2048]{1,0:T(8,128)S(1)} fusion(bf16[3072,2048]{1,0:T(8,128)(2,1)} %param.17, bf16[64,3072]{1,0:T(8,128)(2,1)S(1)} %get-tuple-element.6, f32[3072]{0:T(1024)S(1)} %convert_element_type.74, f32[64]{0:T(128)S(1)} %add_rsqrt_fusion), kind=kOutput, calls=%fused_computation.50 | convolution fusion | flops 806092800 | bytes 13512960 | tf_op jit(solution)/shard_map/dot_general | solution.py:42
  178.4 13.4 %convolution_convert_fusion.1 = bf16[64,3072]{1,0:T(8,128)(2,1)} fusion(bf16[2048,3072]{1,0:T(8,128)(2,1)} %param.19, bf16[3072,2048]{1,0:T(8,128)(2,1)} %param.18, f32[64,2048]{1,0:T(8,128)S(1)} %fusion.38, bf16[64,3072]{1,0:T(8,128)(2,1)S(1)} %get-tuple-element.6, f32[3072]{0:T(1024)S(1)} %convert_element_type.74, f32[64]{0:T(128)S(1)} %add_rsqrt_fusion), kind=kOutput, calls=%fused_computation.12 | convolution fusion | flops 1612382208 | bytes 26489088 | tf_op jit(solution)/shard_map/dot_general | solution.py:54
  191.8 0.0 all-reduce.5.cloned.1.call-update
  191.8 27.2 %all-reduce.5.cloned.1.call-done = bf16[64,3072]{1,0:T(8,128)(2,1)} async-done(((bf16[64,3072]{1,0:T(8,128)(2,1)}), bf16[64,3072]{1,0:T(8,128)(2,1)}) %all-reduce.5.cloned.1.call-update) | async-done | bytes 393232 | tf_op jit(solution)/shard_map/psum | solution.py:49
  219.0 1.8 fusion.19
  (4 shorter events, 0.1 us)
Async XLA Ops:
  6.5 163.6 %all-reduce.3.cloned.1.call-start = ((), (), s32[]{:S(2)}) async-start(), calls=%async_computation | async-start | bytes 786432 | tf_op jit(solution)/shard_map/psum | solution.py:49
  87.6 52.5 %copy-start.1 = (bf16[3072]{0:T(1024)(128)(2,1)S(1)}, bf16[3072]{0:T(1024)(128)(2,1)}, u32[]{:S(2)}) copy-start(bf16[3072]{0:T(1024)(128)(2,1)} %param.16) | copy-start | bytes 18436
  87.6 82.5 %copy-start = (bf16[64,3072]{1,0:T(8,128)(2,1)S(1)}, bf16[64,3072]{1,0:T(8,128)(2,1)}, u32[]{:S(2)}) copy-start(bf16[64,3072]{1,0:T(8,128)(2,1)} %param.10) | copy-start | bytes 1179652
  140.1 78.9 %all-reduce.5.cloned.1.call-start = ((), (), s32[]{:S(2)}) async-start(), calls=%async_computation.1 | async-start | bytes 786432 | tf_op jit(solution)/shard_map/psum | solution.py:49
Sparse Core Ops, SparseCore 0:
  140.2 29.8 all-reduce.2
  191.9 27.0 all-reduce.4
where the time goes:
time: 228 us
  matrix products  138 us (61%)
  waiting for transfers between devices  57.2 us (25%)
  other arithmetic  18 us (8%)
  between operations  13.5 us (6%)
    dot_general x2, matrix products, einsum(): return jnp.einsum(form, a.astype(jnp.float32), b.astype(jnp.float32))  111 us
    psum x2, waiting for transfers between devices, added(): lax.psum(term.astype(jnp.bfloat16), 'tp').astype(jnp.float32)  57.2 us
    dot_general x1, matrix products, step(): jnp.dot(hidden_of(normed(h, gain_m), w_gate, w_up), w_down, preferred_ele...  13.4 us
    sub x1, other arithmetic, seen_by(): weights = jax.nn.softmax(scores, -1).astype(jnp.bfloat16)  12.9 us
    dot_general x1, matrix products, hidden_of(): gate = jnp.dot(b, w_gate, preferred_element_type=jnp.float32)  6.94 us
  transfers between devices with their start and end apart: 2, of which 2 were waited for; matrix products, arithmetic and copies ran while one was open for 0% of the time, Pallas kernels for 0%

commit v1 on v0

v1 whole, which is shorter than its diff:
```python
import functools

import jax
import jax.numpy as jnp
import numpy as np
from jax import lax
from jax.experimental import pallas as pl
from jax.experimental.pallas import tpu as pltpu
from jax.sharding import PartitionSpec as P

MESH = pl.DeviceIdType.MESH
BF16, F32 = jnp.bfloat16, jnp.float32
HEAD = 128
THETA = 10000
SEQS, CACHE, D, FF = 64, 4096, 3072, 2048
HEADS, KV = 6, 2
RING = 4
CHUNK = 512
COLS = 512
HALF = D // 2
BLOCKS = HALF // COLS
FF_BLOCKS = FF // COLS


def dot(a, w):
    return jnp.dot(a, w, preferred_element_type=F32)


def normed(x, gain):
    wide = x.astype(F32)
    scale = lax.rsqrt(jnp.mean(wide * wide, -1, keepdims=True) + 1e-6)
    return (wide * scale * gain.astype(F32)).astype(BF16)


def pair(ref, p, first, rows):
    at = 2 * p * CHUNK + first
    return jnp.concatenate([ref[at : at + rows, :], ref[at + CHUNK : at + CHUNK + rows, :]], 1)


def scores_of(k, q):
    zero = jnp.zeros((8, HEAD), F32)
    two = jnp.concatenate([jnp.concatenate([q, zero], 1), jnp.concatenate([zero, q], 1)], 0).astype(BF16)
    sums = [None, None]
    rows = CHUNK // 2
    for p in range(8):
        above, below = [jnp.zeros((n, 2 * HEAD), BF16) for n in (16 * p, 112 - 16 * p)]
        spread = jnp.concatenate([*([above] if p else []), two, *([below] if p < 7 else [])], 0)
        for h in range(2):
            term = lax.dot_general(pair(k, p, h * rows, rows), spread, (((1,), (1,)), ((), ())), preferred_element_type=F32)
            sums[h] = term if sums[h] is None else sums[h] + term
    return jnp.concatenate(sums, 0).T


def attended(scores, v, seen):
    s = scores.reshape(16, 8, CHUNK)
    s = jnp.where(seen, s, -jnp.inf)
    top = jnp.max(jnp.max(s, 0), 1, keepdims=True)
    e = jnp.exp2((s - top[None]) * (HEAD**-0.5 * 1.4426950408889634))
    total = jnp.sum(jnp.sum(e, 0), 1, keepdims=True)
    w = (e * (1.0 / total)[None]).reshape(128, CHUNK).astype(BF16)
    sums = [None, None]
    rows = CHUNK // 2
    for p in range(8):
        for h in range(2):
            term = dot(w[16 * p : 16 * p + 16, h * rows : h * rows + rows], pair(v, p, h * rows, rows))
            sums[h] = term if sums[h] is None else sums[h] + term
    both = sums[0] + sums[1]
    return both[:8, :HEAD] + both[8:, HEAD:]


def kernel(
    x_hbm, k_hbm, v_hbm, ga_hbm, wq_hbm, wo_hbm, gm_hbm, wg_hbm, wu_hbm, wd_hbm, turn_hbm,
    y_hbm,
    x, ga, gm, turn, kbuf, vbuf, wo, wg, wu, wd, q, o, scores, h, hidden, y,
    half_out, half_in, chip_out, chip_in,
    ksem, vsem, small_sem, wq_sem, wo_sem, wg_sem, wu_sem, wd_sem, y_sem, send_sem, recv_sem,
):
    me = lax.axis_index("tp")
    core = lax.rem(me, 2)
    partner = me + 1 - 2 * core
    across = lax.rem(me + 2, 4)
    own, other = core * HALF, (1 - core) * HALF

    def columns(start, i):
        return pl.ds(pl.multiple_of(start + i * COLS, COLS), COLS)

    small = [
        pltpu.make_async_copy(a, b, small_sem.at[i])
        for i, (a, b) in enumerate(((x_hbm, x), (ga_hbm, ga), (gm_hbm, gm), (turn_hbm, turn)))
    ]
    wq_copies = [
        pltpu.make_async_copy(wq_hbm.at[:, 0:512], wg.at[2], wq_sem.at[0]),
        pltpu.make_async_copy(wq_hbm.at[:, 512:768], wg.at[3, :, 0:256], wq_sem.at[1]),
    ]

    def k_copy(t):
        return pltpu.make_async_copy(k_hbm.at[t], kbuf.at[lax.rem(t, RING)], ksem.at[lax.rem(t, RING)])

    def v_copy(t):
        return pltpu.make_async_copy(v_hbm.at[t], vbuf.at[lax.rem(t, RING)], vsem.at[lax.rem(t, RING)])

    wo_copies, wd_copies = [
        [
            pltpu.make_async_copy(hbm.at[:, columns(other if i < BLOCKS else own, i % BLOCKS)], buf.at[i], sem.at[i])
            for i in range(2 * BLOCKS)
        ]
        for hbm, buf, sem in ((wo_hbm, wo, wo_sem), (wd_hbm, wd, wd_sem))
    ]
    wg_copies, wu_copies = [
        [pltpu.make_async_copy(hbm.at[:, i * COLS : (i + 1) * COLS], buf.at[i], sem.at[i]) for i in range(FF_BLOCKS)]
        for hbm, buf, sem in ((wg_hbm, wg, wg_sem), (wu_hbm, wu, wu_sem))
    ]

    for c in (*small, *wq_copies):
        c.start()
    for t in range(RING):
        k_copy(jnp.int32(t)).start()
        v_copy(jnp.int32(t)).start()

    barrier = pltpu.get_barrier_semaphore()
    for d in (partner, across):
        pl.semaphore_signal(barrier, inc=1, device_id={"tp": d}, device_id_type=MESH)

    for c in small:
        c.wait()
    a = normed(x[...], ga[...])
    for c in wq_copies:
        c.wait()
    projected = jnp.concatenate([dot(a, wg[2]), dot(a, wg[3, :, 0:256])], 1).astype(BF16).astype(F32)
    cos, sin = turn[0:1, :], turn[1:2, :]
    for i in range(HEADS):
        t = projected[:, i * HEAD : (i + 1) * HEAD]
        q[:, i, :] = (t * cos + pltpu.roll(t, HEAD // 2, 1) * sin).astype(BF16).astype(F32)
    for i in range(HEADS, 8):
        q[:, i, :] = jnp.zeros((SEQS, HEAD), F32)

    row = lax.broadcasted_iota(jnp.int32, (8, CHUNK), 0)
    odd = lax.broadcasted_iota(jnp.int32, (8, CHUNK), 1) % 2
    seen = (((row < 3) & (odd == 0)) | ((row >= 3) & (row < 6) & (odd == 1)) | (row >= 6))[None]

    first = jnp.int32(0)
    k_copy(first).wait()
    scores[...] = scores_of(kbuf.at[0], q[0])
    k_copy(first + RING).start()

    def step(t, _):
        k_copy(t + 1).wait()
        v_copy(t).wait()
        before = scores[...]
        after = scores_of(kbuf.at[lax.rem(t + 1, RING)], q[t + 1])
        o[t] = attended(before, vbuf.at[lax.rem(t, RING)], seen)
        scores[...] = after

        @pl.when(t + RING < SEQS)
        def _():
            v_copy(t + RING).start()

            @pl.when(t + 1 + RING < SEQS)
            def _():
                k_copy(t + 1 + RING).start()

        @pl.when(t == SEQS - RING)
        def _():
            for c in (*wo_copies, *(c for two in zip(wg_copies, wu_copies) for c in two), *wd_copies):
                c.start()

        return 0

    lax.fori_loop(0, SEQS - 1, step, 0)
    last = jnp.int32(SEQS - 1)
    v_copy(last).wait()
    o[SEQS - 1] = attended(scores[...], vbuf.at[RING - 1], seen)

    pl.semaphore_wait(barrier, 2)

    def added(which, lhs, w, w_copies, base, out, out_other, keep):
        def remote(phase, i, src, dst, device):
            return pltpu.make_async_remote_copy(
                src_ref=src, dst_ref=dst, send_sem=send_sem.at[which, phase, i], recv_sem=recv_sem.at[which, phase, i],
                device_id={"tp": device}, device_id_type=MESH,
            )

        halves = [remote(0, i, half_out.at[which, i], half_in.at[which, i], partner) for i in range(BLOCKS)]
        chips = [remote(1, i, chip_out.at[which, i], chip_in.at[which, i], across) for i in range(BLOCKS)]
        finals = [remote(2, i, out.at[:, columns(own, i)], out_other.at[:, columns(own, i)], partner) for i in range(BLOCKS)]
        for i in range(BLOCKS):
            w_copies[i].wait()
            half_out[which, i] = dot(lhs, w[i]).astype(BF16)
            halves[i].start()
        for i in range(BLOCKS):
            w_copies[BLOCKS + i].wait()
            term = dot(lhs, w[BLOCKS + i])
            halves[i].wait_recv()
            chip_out[which, i] = (term + half_in[which, i].astype(F32)).astype(BF16)
            chips[i].start()
        for i in range(BLOCKS):
            chips[i].wait_recv()
            total = chip_out[which, i].astype(F32) + chip_in[which, i].astype(F32)
            out[:, columns(own, i)] = (base[:, columns(own, i)].astype(F32) + total).astype(BF16)
            finals[i].start()
            keep(i)
        for c in finals:
            c.wait()
        for c in (*halves, *chips):
            c.wait_send()

    attention = jnp.concatenate([o[:, i, :] for i in range(HEADS)], 1).astype(BF16)
    added(0, attention, wo, wo_copies, x, h, h, lambda i: None)

    b = normed(h[...], gm[...])
    for i in range(FF_BLOCKS):
        wg_copies[i].wait()
        wu_copies[i].wait()
        gate = dot(b, wg[i])
        up = dot(b, wu[i])
        hidden[:, i * COLS : (i + 1) * COLS] = (gate * lax.logistic(gate) * up).astype(BF16)

    y_copies = [
        pltpu.make_async_copy(y.at[:, columns(own, i)], y_hbm.at[:, columns(own, i)], y_sem.at[i]) for i in range(BLOCKS)
    ]
    added(1, hidden[...], wd, wd_copies, h, y, y_hbm, lambda i: y_copies[i].start())
    for c in y_copies:
        c.wait()


def layer(x, k_cache, v_cache, gain_a, wq, wo, gain_m, w_gate, w_up, w_down):
    half = HEAD // 2
    angle = np.float32(CACHE - 1) * np.float32(THETA) ** (-np.arange(half, dtype=np.float32) / np.float32(half))
    cos, sin = np.cos(angle), np.sin(angle)
    turn = jnp.asarray(np.stack([np.concatenate([cos, cos]), np.concatenate([-sin, sin])]).astype(np.float32))
    k, v = (c.reshape(SEQS, CACHE * KV, HEAD) for c in (k_cache, v_cache))
    vmem, dma = pltpu.VMEM, pltpu.SemaphoreType.DMA
    return pl.pallas_call(
        kernel,
        out_shape=jax.ShapeDtypeStruct((SEQS, D), BF16),
        in_specs=[pl.BlockSpec(memory_space=pl.ANY)] * 11,
        out_specs=pl.BlockSpec(memory_space=pl.ANY),
        scratch_shapes=[
            vmem((SEQS, D), BF16),
            vmem((1, D), BF16),
            vmem((1, D), BF16),
            vmem((2, HEAD), F32),
            vmem((RING, CACHE * KV, HEAD), BF16),
            vmem((RING, CACHE * KV, HEAD), BF16),
            vmem((2 * BLOCKS, HEADS * HEAD, COLS), BF16),
            vmem((FF_BLOCKS, D, COLS), BF16),
            vmem((FF_BLOCKS, D, COLS), BF16),
            vmem((2 * BLOCKS, FF, COLS), BF16),
            vmem((SEQS, 8, HEAD), F32),
            vmem((SEQS, 8, HEAD), F32),
            vmem((HEAD, CHUNK), F32),
            vmem((SEQS, D), BF16),
            vmem((SEQS, FF), BF16),
            vmem((SEQS, D), BF16),
            *[vmem((2, BLOCKS, SEQS, COLS), BF16)] * 4,
            dma((RING,)),
            dma((RING,)),
            dma((4,)),
            dma((2,)),
            dma((2 * BLOCKS,)),
            dma((FF_BLOCKS,)),
            dma((FF_BLOCKS,)),
            dma((2 * BLOCKS,)),
            dma((BLOCKS,)),
            dma((2, 3, BLOCKS)),
            dma((2, 3, BLOCKS)),
        ],
        compiler_params=pltpu.CompilerParams(collective_id=0, has_side_effects=True, vmem_limit_bytes=67_043_328),
    )(x, k, v, gain_a.reshape(1, D), wq, wo, gain_m.reshape(1, D), w_gate, w_up, w_down, turn)


def solution(mesh):
    states, cache, columns, rows_of = P("dp", None), P("dp", None, "tp", None), P(None, "tp"), P("tp", None)
    return jax.shard_map(
        layer,
        mesh=mesh,
        in_specs=(states, cache, cache, P(None), columns, rows_of, P(None), columns, columns, rows_of),
        out_specs=states,
        check_vma=False,
    )
```

time: 228 us -> 117 us (0.51)
  matrix products: 138 us -> 0 us
  Pallas kernels: 0 us -> 112 us
  waiting for transfers between devices: 57.2 us -> 0 us
  other arithmetic: 18 us -> 0 us
  between operations: 13.5 us -> 0.01 us
  local copies, waits for them, and re-layouts: 0.52 us -> 4.36 us
    dot_general x6 -> x0, matrix products: 138 us -> none  [the longest x2 111 us: einsum(): return jnp.einsum(form, a.astype(jnp.float32), b.astype(jnp.float32))]
    pallas_call x0 -> x1, Pallas kernels: none -> 112 us  [layer(): pl.pallas_call(kernel, out_shape=jax.ShapeDtypeStruct((SEQS, D), BF16), i...]
    psum x2 -> x0, waiting for transfers between devices: 57.2 us -> none  [added(): lax.psum(term.astype(jnp.bfloat16), 'tp').astype(jnp.float32)]
    sub x1 -> x0, other arithmetic: 12.9 us -> none  [seen_by(): weights = jax.nn.softmax(scores, -1).astype(jnp.bfloat16)]
    convert_element_type x3 -> x0, other arithmetic: 2.54 us -> none  [the longest x1 1.83 us: added(): (t.astype(jnp.float32) + lax.psum(term.astype(jnp.bfloat16), 'tp').astype...]
    reduce_sum x2 -> x0, other arithmetic: 2.41 us -> none  [normed(): scale = lax.rsqrt(jnp.mean(wide * wide, -1, keepdims=True) + 1e-06)]
    reshape x2, local copies, waits for them, and re-layouts: 0.22 us -> 2.59 us  [the longest x1 1.3 us: layer(): gain_a.reshape(1, D)]
  transfers between devices with their start and end apart: 2 -> 0, of which waited for: 2 -> 0; matrix products, arithmetic and copies ran while one was open for 0% -> 0% of each run, Pallas kernels for 0% -> 0%
where the time goes in v1:
time: 117 us
  Pallas kernels  112 us (96%)
  local copies, waits for them, and re-layouts  4.36 us (4%)
    pallas_call x1, Pallas kernels, layer(): pl.pallas_call(kernel, out_shape=jax.ShapeDtypeStruct((SEQS, D), BF16), i...  112 us

profile of v1, /device:TPU:0, one launch (start us, length us, event | category | flops | bytes accessed | tf_op | source)
XLA Modules:
  0.0 116.8 jit_solution(6937772274020866983)
XLA Ops:
  0.0 1.3 %reshape.14.ga_hbm = bf16[1,3072]{1,0:T(2,128)(2,1)} reshape(bf16[3072]{0:T(1024)(128)(2,1)} %param.14) | data formatting | bytes 12288 | tf_op jit(solution)/shard_map/reshape | solution.py:269
  1.3 1.3 %reshape.15.gm_hbm = bf16[1,3072]{1,0:T(2,128)(2,1)} reshape(bf16[3072]{0:T(1024)(128)(2,1)} %param.17) | data formatting | bytes 12288 | tf_op jit(solution)/shard_map/reshape | solution.py:269
  2.6 112.4 %shard_map.109 = bf16[64,3072]{1,0:T(8,128)(2,1)} custom-call(bf16[64,3072]{1,0:T(8,128)(2,1)} %x_hbm.1, bf16[64,8192,128]{2,1,0:T(8,128)(2,1)} %bitcast.k_hbm, bf16[64,8192,128]{2,1,0:T(8,128)(2,1)} %bitcast.1.v_hbm, bf16[1,3072]{1,0:T(2,128)(2,1)} %reshape.14.ga_hbm, bf16[3072,768]{1,0:T(8,128)(2,1)} %wq_hbm.1, bf16[768,3072]{1,0:T(8,128)(2,1)} %wo_hbm.1, ...), custom_call_target="tpu_custom_call" | custom-call | tf_op jit(solution)/shard_map/pallas_call | solution.py:233
  115.0 1.8 %copy.13 = bf16[64,3072]{1,0:T(8,128)(2,1)} copy(bf16[64,3072]{1,0:T(8,128)(2,1)} %shard_map.109) | data formatting | bytes 786432

commit v2 on v1

--- a/solution.py
+++ b/solution.py
@@ -20,6 +20,7 @@
 HALF = D // 2
 BLOCKS = HALF // COLS
 FF_BLOCKS = FF // COLS
+EARLY = 48
 
 
 def dot(a, w):
@@ -29,7 +30,7 @@
 def normed(x, gain):
     wide = x.astype(F32)
     scale = lax.rsqrt(jnp.mean(wide * wide, -1, keepdims=True) + 1e-6)
-    return (wide * scale * gain.astype(F32)).astype(BF16)
+    return (wide * scale * gain.astype(F32).reshape(1, D)).astype(BF16)
 
 
 def pair(ref, p, first, rows):
@@ -111,11 +112,58 @@
         for hbm, buf, sem in ((wg_hbm, wg, wg_sem), (wu_hbm, wu, wu_sem))
     ]
 
+    def remote(which, phase, i, src, dst, device):
+        return pltpu.make_async_remote_copy(
+            src_ref=src, dst_ref=dst, send_sem=send_sem.at[which, phase, i], recv_sem=recv_sem.at[which, phase, i],
+            device_id={"tp": device}, device_id_type=MESH,
+        )
+
+    class Sum:
+        def __init__(self, which, at, first, rows, w, base, out, out_other):
+            self.at, self.w, self.base, self.out, self.rows = at, w, base, out, pl.ds(first, rows)
+            r = self.rows
+            self.halves = [remote(which, 0, i, half_out.at[at, i, r], half_in.at[at, i, r], partner) for i in range(BLOCKS)]
+            self.chips = [remote(which, 1, i, chip_out.at[at, i, r], chip_in.at[at, i, r], across) for i in range(BLOCKS)]
+            self.finals = [
+                remote(which, 2, i, out.at[r, columns(own, i)], out_other.at[r, columns(own, i)], partner) for i in range(BLOCKS)
+            ]
+
+        def swap_halves(self, lhs, ready=lambda i: None):
+            for i in range(BLOCKS):
+                ready(i)
+                half_out[self.at, i, self.rows] = dot(lhs, self.w[i]).astype(BF16)
+                self.halves[i].start()
+
+        def swap_chips(self, lhs, ready=lambda i: None):
+            for i in range(BLOCKS):
+                ready(BLOCKS + i)
+                term = dot(lhs, self.w[BLOCKS + i])
+                self.halves[i].wait_recv()
+                chip_out[self.at, i, self.rows] = (term + half_in[self.at, i, self.rows].astype(F32)).astype(BF16)
+                self.chips[i].start()
+
+        def swap_finals(self, keep=lambda i: None):
+            for i in range(BLOCKS):
+                self.chips[i].wait_recv()
+                total = chip_out[self.at, i, self.rows].astype(F32) + chip_in[self.at, i, self.rows].astype(F32)
+                cols = columns(own, i)
+                self.out[self.rows, cols] = (self.base[self.rows, cols].astype(F32) + total).astype(BF16)
+                self.finals[i].start()
+                keep(i)
+
+        def finish(self):
+            for c in self.finals:
+                c.wait()
+            for c in (*self.halves, *self.chips):
+                c.wait_send()
+
     for c in (*small, *wq_copies):
         c.start()
     for t in range(RING):
         k_copy(jnp.int32(t)).start()
         v_copy(jnp.int32(t)).start()
+    for c in wo_copies:
+        c.start()
 
     barrier = pltpu.get_barrier_semaphore()
     for d in (partner, across):
@@ -143,6 +191,11 @@
     scores[...] = scores_of(kbuf.at[0], q[0])
     k_copy(first + RING).start()
 
+    def attention_of(first, rows):
+        return jnp.concatenate([o[first : first + rows, i, :] for i in range(HEADS)], 1).astype(BF16)
+
+    early, late = [Sum(which, 0, first, rows, wo, x, h, h) for which, first, rows in ((0, 0, EARLY), (1, EARLY, SEQS - EARLY))]
+
     def step(t, _):
         k_copy(t + 1).wait()
         v_copy(t).wait()
@@ -161,8 +214,28 @@
 
         @pl.when(t == SEQS - RING)
         def _():
-            for c in (*wo_copies, *(c for two in zip(wg_copies, wu_copies) for c in two), *wd_copies):
+            for c in (*(c for two in zip(wg_copies, wu_copies) for c in two), *wd_copies):
                 c.start()
+
+        @pl.when(t == EARLY)
+        def _():
+            pl.semaphore_wait(barrier, 2)
+            for c in wo_copies:
+                c.wait()
+            early.swap_halves(attention_of(0, EARLY))
+
+        @pl.when(t == EARLY + 2)
+        def _():
+            early.swap_chips(attention_of(0, EARLY))
+
+        @pl.when(t == EARLY + 6)
+        def _():
+            early.swap_finals()
+
+        @pl.when(t == EARLY + 9)
+        def _():
+            early.finish()
+            y[:EARLY] = normed(h[:EARLY], gm[...])
 
         return 0
 
@@ -171,54 +244,29 @@
     v_copy(last).wait()
     o[SEQS - 1] = attended(scores[...], vbuf.at[RING - 1], seen)
 
-    pl.semaphore_wait(barrier, 2)
-
-    def added(which, lhs, w, w_copies, base, out, out_other, keep):
-        def remote(phase, i, src, dst, device):
-            return pltpu.make_async_remote_copy(
-                src_ref=src, dst_ref=dst, send_sem=send_sem.at[which, phase, i], recv_sem=recv_sem.at[which, phase, i],
-                device_id={"tp": device}, device_id_type=MESH,
-            )
-
-        halves = [remote(0, i, half_out.at[which, i], half_in.at[which, i], partner) for i in range(BLOCKS)]
-        chips = [remote(1, i, chip_out.at[which, i], chip_in.at[which, i], across) for i in range(BLOCKS)]
-        finals = [remote(2, i, out.at[:, columns(own, i)], out_other.at[:, columns(own, i)], partner) for i in range(BLOCKS)]
-        for i in range(BLOCKS):
-            w_copies[i].wait()
-            half_out[which, i] = dot(lhs, w[i]).astype(BF16)
-            halves[i].start()
-        for i in range(BLOCKS):
-            w_copies[BLOCKS + i].wait()
-            term = dot(lhs, w[BLOCKS + i])
-            halves[i].wait_recv()
-            chip_out[which, i] = (term + half_in[which, i].astype(F32)).astype(BF16)
-            chips[i].start()
-        for i in range(BLOCKS):
-            chips[i].wait_recv()
-            total = chip_out[which, i].astype(F32) + chip_in[which, i].astype(F32)
-            out[:, columns(own, i)] = (base[:, columns(own, i)].astype(F32) + total).astype(BF16)
-            finals[i].start()
-            keep(i)
-        for c in finals:
-            c.wait()
-        for c in (*halves, *chips):
-            c.wait_send()
-
-    attention = jnp.concatenate([o[:, i, :] for i in range(HEADS)], 1).astype(BF16)
-    added(0, attention, wo, wo_copies, x, h, h, lambda i: None)
-
-    b = normed(h[...], gm[...])
+
+    attention = attention_of(EARLY, SEQS - EARLY)
+    late.swap_halves(attention)
+    late.swap_chips(attention)
+    late.swap_finals()
+    late.finish()
+    y[EARLY:] = normed(h[EARLY:], gm[...])
+
     for i in range(FF_BLOCKS):
         wg_copies[i].wait()
         wu_copies[i].wait()
-        gate = dot(b, wg[i])
-        up = dot(b, wu[i])
+        gate = dot(y[...], wg[i])
+        up = dot(y[...], wu[i])
         hidden[:, i * COLS : (i + 1) * COLS] = (gate * lax.logistic(gate) * up).astype(BF16)
 
+    mlp = Sum(2, 1, 0, SEQS, wd, h, y, y_hbm)
     y_copies = [
         pltpu.make_async_copy(y.at[:, columns(own, i)], y_hbm.at[:, columns(own, i)], y_sem.at[i]) for i in range(BLOCKS)
     ]
-    added(1, hidden[...], wd, wd_copies, h, y, y_hbm, lambda i: y_copies[i].start())
+    mlp.swap_halves(hidden[...], lambda i: wd_copies[i].wait())
+    mlp.swap_chips(hidden[...], lambda i: wd_copies[i].wait())
+    mlp.swap_finals(lambda i: y_copies[i].start())
+    mlp.finish()
     for c in y_copies:
         c.wait()
 
@@ -237,8 +285,8 @@
         out_specs=pl.BlockSpec(memory_space=pl.ANY),
         scratch_shapes=[
             vmem((SEQS, D), BF16),
-            vmem((1, D), BF16),
-            vmem((1, D), BF16),
+            vmem((D,), BF16),
+            vmem((D,), BF16),
             vmem((2, HEAD), F32),
             vmem((RING, CACHE * KV, HEAD), BF16),
             vmem((RING, CACHE * KV, HEAD), BF16),
@@ -262,11 +310,11 @@
             dma((FF_BLOCKS,)),
             dma((2 * BLOCKS,)),
             dma((BLOCKS,)),
-            dma((2, 3, BLOCKS)),
-            dma((2, 3, BLOCKS)),
+            dma((3, 3, BLOCKS)),
+            dma((3, 3, BLOCKS)),
         ],
         compiler_params=pltpu.CompilerParams(collective_id=0, has_side_effects=True, vmem_limit_bytes=67_043_328),
-    )(x, k, v, gain_a.reshape(1, D), wq, wo, gain_m.reshape(1, D), w_gate, w_up, w_down, turn)
+    )(x, k, v, gain_a, wq, wo, gain_m, w_gate, w_up, w_down, turn)
 
 
 def solution(mesh):

time: 117 us -> 109 us (0.932)
  Pallas kernels: 112 us -> 107 us
  local copies, waits for them, and re-layouts: 4.36 us -> 1.77 us
    pallas_call x1, Pallas kernels: 112 us -> 107 us  [layer(): pl.pallas_call(kernel, out_shape=jax.ShapeDtypeStruct((SEQS, D), BF16), i...]
    reshape x2 -> x0, local copies, waits for them, and re-layouts: 2.59 us -> none  [the longest x1 1.3 us: layer(): gain_a.reshape(1, D)]
where the time goes in v2:
time: 109 us
  Pallas kernels  107 us (98%)
  local copies, waits for them, and re-layouts  1.77 us (2%)
    pallas_call x1, Pallas kernels, layer(): pl.pallas_call(kernel, out_shape=jax.ShapeDtypeStruct((SEQS, D), BF16), i...  107 us

profile of v2, /device:TPU:0, one launch (start us, length us, event | category | flops | bytes accessed | tf_op | source)
XLA Modules:
  0.0 109.2 jit_solution(3580136663032880356)
XLA Ops:
  0.0 107.4 %shard_map.109 = bf16[64,3072]{1,0:T(8,128)(2,1)} custom-call(bf16[64,3072]{1,0:T(8,128)(2,1)} %x_hbm.1, bf16[64,8192,128]{2,1,0:T(8,128)(2,1)} %bitcast.k_hbm, bf16[64,8192,128]{2,1,0:T(8,128)(2,1)} %bitcast.1.v_hbm, bf16[3072]{0:T(1024)(128)(2,1)} %ga_hbm.1, bf16[3072,768]{1,0:T(8,128)(2,1)} %wq_hbm.1, bf16[768,3072]{1,0:T(8,128)(2,1)} %wo_hbm.1, ...), custom_call_target="tpu_custom_call" | custom-call | tf_op jit(solution)/shard_map/pallas_call | solution.py:281
  107.4 1.8 %copy.13 = bf16[64,3072]{1,0:T(8,128)(2,1)} copy(bf16[64,3072]{1,0:T(8,128)(2,1)} %shard_map.109) | data formatting | bytes 786432

commit v3 on v2

--- a/solution.py
+++ b/solution.py
@@ -72,7 +72,7 @@
 def kernel(
     x_hbm, k_hbm, v_hbm, ga_hbm, wq_hbm, wo_hbm, gm_hbm, wg_hbm, wu_hbm, wd_hbm, turn_hbm,
     y_hbm,
-    x, ga, gm, turn, kbuf, vbuf, wo, wg, wu, wd, q, o, scores, h, hidden, y,
+    x, ga, gm, turn, kbuf, vbuf, wo, wg, wu, wd, q, o, scores, attention, h, hidden, y,
     half_out, half_in, chip_out, chip_in,
     ksem, vsem, small_sem, wq_sem, wo_sem, wg_sem, wu_sem, wd_sem, y_sem, send_sem, recv_sem,
 ):
@@ -100,70 +100,92 @@
     def v_copy(t):
         return pltpu.make_async_copy(v_hbm.at[t], vbuf.at[lax.rem(t, RING)], vsem.at[lax.rem(t, RING)])
 
-    wo_copies, wd_copies = [
-        [
-            pltpu.make_async_copy(hbm.at[:, columns(other if i < BLOCKS else own, i % BLOCKS)], buf.at[i], sem.at[i])
-            for i in range(2 * BLOCKS)
-        ]
-        for hbm, buf, sem in ((wo_hbm, wo, wo_sem), (wd_hbm, wd, wd_sem))
-    ]
-    wg_copies, wu_copies = [
-        [pltpu.make_async_copy(hbm.at[:, i * COLS : (i + 1) * COLS], buf.at[i], sem.at[i]) for i in range(FF_BLOCKS)]
-        for hbm, buf, sem in ((wg_hbm, wg, wg_sem), (wu_hbm, wu, wu_sem))
-    ]
-
-    def remote(which, phase, i, src, dst, device):
-        return pltpu.make_async_remote_copy(
-            src_ref=src, dst_ref=dst, send_sem=send_sem.at[which, phase, i], recv_sem=recv_sem.at[which, phase, i],
-            device_id={"tp": device}, device_id_type=MESH,
-        )
+    def block_copy(hbm, buf, sem):
+        def copy(i):
+            start = pl.multiple_of(jnp.where(i < BLOCKS, other, own) + lax.rem(i, BLOCKS) * COLS, COLS)
+            return pltpu.make_async_copy(hbm.at[:, pl.ds(start, COLS)], buf.at[i], sem.at[i])
+
+        return copy
+
+    def ff_copy(hbm, buf, sem):
+        def copy(i):
+            return pltpu.make_async_copy(hbm.at[:, pl.ds(pl.multiple_of(i * COLS, COLS), COLS)], buf.at[i], sem.at[i])
+
+        return copy
+
+    wo_copy, wd_copy = block_copy(wo_hbm, wo, wo_sem), block_copy(wd_hbm, wd, wd_sem)
+    wg_copy, wu_copy = ff_copy(wg_hbm, wg, wg_sem), ff_copy(wu_hbm, wu, wu_sem)
+
+    def loop(n, body):
+        def one(i, _):
+            body(i)
+            return 0
+
+        lax.fori_loop(0, n, one, 0)
 
     class Sum:
         def __init__(self, which, at, first, rows, w, base, out, out_other):
-            self.at, self.w, self.base, self.out, self.rows = at, w, base, out, pl.ds(first, rows)
-            r = self.rows
-            self.halves = [remote(which, 0, i, half_out.at[at, i, r], half_in.at[at, i, r], partner) for i in range(BLOCKS)]
-            self.chips = [remote(which, 1, i, chip_out.at[at, i, r], chip_in.at[at, i, r], across) for i in range(BLOCKS)]
-            self.finals = [
-                remote(which, 2, i, out.at[r, columns(own, i)], out_other.at[r, columns(own, i)], partner) for i in range(BLOCKS)
-            ]
+            self.which, self.at, self.w, self.base, self.out, self.out_other = which, at, w, base, out, out_other
+            self.rows = pl.ds(first, rows)
+
+        def remote(self, phase, i, src, dst, device):
+            return pltpu.make_async_remote_copy(
+                src_ref=src, dst_ref=dst, send_sem=send_sem.at[self.which, phase, i], recv_sem=recv_sem.at[self.which, phase, i],
+                device_id={"tp": device}, device_id_type=MESH,
+            )
+
+        def half(self, i):
+            return self.remote(0, i, half_out.at[self.at, i, self.rows], half_in.at[self.at, i, self.rows], partner)
+
+        def chip(self, i):
+            return self.remote(1, i, chip_out.at[self.at, i, self.rows], chip_in.at[self.at, i, self.rows], across)
+
+        def final(self, i):
+            return self.remote(2, i, self.out.at[self.rows, columns(own, i)], self.out_other.at[self.rows, columns(own, i)], partner)
 
         def swap_halves(self, lhs, ready=lambda i: None):
-            for i in range(BLOCKS):
+            def body(i):
                 ready(i)
-                half_out[self.at, i, self.rows] = dot(lhs, self.w[i]).astype(BF16)
-                self.halves[i].start()
+                half_out[self.at, i, self.rows] = dot(lhs(), self.w[i]).astype(BF16)
+                self.half(i).start()
+
+            loop(BLOCKS, body)
 
         def swap_chips(self, lhs, ready=lambda i: None):
-            for i in range(BLOCKS):
+            def body(i):
                 ready(BLOCKS + i)
-                term = dot(lhs, self.w[BLOCKS + i])
-                self.halves[i].wait_recv()
+                term = dot(lhs(), self.w[BLOCKS + i])
+                self.half(i).wait_recv()
                 chip_out[self.at, i, self.rows] = (term + half_in[self.at, i, self.rows].astype(F32)).astype(BF16)
-                self.chips[i].start()
+                self.chip(i).start()
+
+            loop(BLOCKS, body)
 
         def swap_finals(self, keep=lambda i: None):
-            for i in range(BLOCKS):
-                self.chips[i].wait_recv()
+            def body(i):
+                self.chip(i).wait_recv()
                 total = chip_out[self.at, i, self.rows].astype(F32) + chip_in[self.at, i, self.rows].astype(F32)
                 cols = columns(own, i)
                 self.out[self.rows, cols] = (self.base[self.rows, cols].astype(F32) + total).astype(BF16)
-                self.finals[i].start()
+                self.final(i).start()
                 keep(i)
 
+            loop(BLOCKS, body)
+
         def finish(self):
-            for c in self.finals:
-                c.wait()
-            for c in (*self.halves, *self.chips):
-                c.wait_send()
+            def body(i):
+                self.final(i).wait()
+                self.half(i).wait_send()
+                self.chip(i).wait_send()
+
+            loop(BLOCKS, body)
 
     for c in (*small, *wq_copies):
         c.start()
     for t in range(RING):
         k_copy(jnp.int32(t)).start()
         v_copy(jnp.int32(t)).start()
-    for c in wo_copies:
-        c.start()
+    loop(2 * BLOCKS, lambda i: wo_copy(i).start())
 
     barrier = pltpu.get_barrier_semaphore()
     for d in (partner, across):
@@ -197,10 +219,13 @@
     early, late = [Sum(which, 0, first, rows, wo, x, h, h) for which, first, rows in ((0, 0, EARLY), (1, EARLY, SEQS - EARLY))]
 
     def step(t, _):
-        k_copy(t + 1).wait()
+        @pl.when(t + 1 < SEQS)
+        def _():
+            k_copy(t + 1).wait()
+
         v_copy(t).wait()
         before = scores[...]
-        after = scores_of(kbuf.at[lax.rem(t + 1, RING)], q[t + 1])
+        after = scores_of(kbuf.at[lax.rem(t + 1, RING)], q[jnp.minimum(t + 1, SEQS - 1)])
         o[t] = attended(before, vbuf.at[lax.rem(t, RING)], seen)
         scores[...] = after
 
@@ -214,61 +239,62 @@
 
         @pl.when(t == SEQS - RING)
         def _():
-            for c in (*(c for two in zip(wg_copies, wu_copies) for c in two), *wd_copies):
-                c.start()
+            def both(i):
+                wg_copy(i).start()
+                wu_copy(i).start()
+
+            loop(FF_BLOCKS, both)
+            loop(2 * BLOCKS, lambda i: wd_copy(i).start())
 
         @pl.when(t == EARLY)
         def _():
             pl.semaphore_wait(barrier, 2)
-            for c in wo_copies:
-                c.wait()
-            early.swap_halves(attention_of(0, EARLY))
+            loop(2 * BLOCKS, lambda i: wo_copy(i).wait())
+            attention[:EARLY] = attention_of(0, EARLY)
+            early.swap_halves(lambda: attention[:EARLY])
 
         @pl.when(t == EARLY + 2)
         def _():
-            early.swap_chips(attention_of(0, EARLY))
-
-        @pl.when(t == EARLY + 6)
+            early.swap_chips(lambda: attention[:EARLY])
+
+        @pl.when(t == EARLY + 7)
         def _():
             early.swap_finals()
 
-        @pl.when(t == EARLY + 9)
+        @pl.when(t == EARLY + 10)
         def _():
             early.finish()
-            y[:EARLY] = normed(h[:EARLY], gm[...])
 
         return 0
 
-    lax.fori_loop(0, SEQS - 1, step, 0)
-    last = jnp.int32(SEQS - 1)
-    v_copy(last).wait()
-    o[SEQS - 1] = attended(scores[...], vbuf.at[RING - 1], seen)
-
-
-    attention = attention_of(EARLY, SEQS - EARLY)
-    late.swap_halves(attention)
-    late.swap_chips(attention)
+    lax.fori_loop(0, SEQS, step, 0)
+
+    attention[EARLY:] = attention_of(EARLY, SEQS - EARLY)
+    late.swap_halves(lambda: attention[EARLY:])
+    late.swap_chips(lambda: attention[EARLY:])
+    y[:EARLY] = normed(h[:EARLY], gm[...])
     late.swap_finals()
     late.finish()
     y[EARLY:] = normed(h[EARLY:], gm[...])
 
-    for i in range(FF_BLOCKS):
-        wg_copies[i].wait()
-        wu_copies[i].wait()
+    def ff(i):
+        wg_copy(i).wait()
+        wu_copy(i).wait()
         gate = dot(y[...], wg[i])
         up = dot(y[...], wu[i])
-        hidden[:, i * COLS : (i + 1) * COLS] = (gate * lax.logistic(gate) * up).astype(BF16)
+        hidden[:, pl.ds(pl.multiple_of(i * COLS, COLS), COLS)] = (gate * lax.logistic(gate) * up).astype(BF16)
+
+    loop(FF_BLOCKS, ff)
+
+    def y_copy(i):
+        return pltpu.make_async_copy(y.at[:, columns(own, i)], y_hbm.at[:, columns(own, i)], y_sem.at[i])
 
     mlp = Sum(2, 1, 0, SEQS, wd, h, y, y_hbm)
-    y_copies = [
-        pltpu.make_async_copy(y.at[:, columns(own, i)], y_hbm.at[:, columns(own, i)], y_sem.at[i]) for i in range(BLOCKS)
-    ]
-    mlp.swap_halves(hidden[...], lambda i: wd_copies[i].wait())
-    mlp.swap_chips(hidden[...], lambda i: wd_copies[i].wait())
-    mlp.swap_finals(lambda i: y_copies[i].start())
+    mlp.swap_halves(lambda: hidden[...], lambda i: wd_copy(i).wait())
+    mlp.swap_chips(lambda: hidden[...], lambda i: wd_copy(i).wait())
+    mlp.swap_finals(lambda i: y_copy(i).start())
     mlp.finish()
-    for c in y_copies:
-        c.wait()
+    loop(BLOCKS, lambda i: y_copy(i).wait())
 
 
 def layer(x, k_cache, v_cache, gain_a, wq, wo, gain_m, w_gate, w_up, w_down):
@@ -297,6 +323,7 @@
             vmem((SEQS, 8, HEAD), F32),
             vmem((SEQS, 8, HEAD), F32),
             vmem((HEAD, CHUNK), F32),
+            vmem((SEQS, HEADS * HEAD), BF16),
             vmem((SEQS, D), BF16),
             vmem((SEQS, FF), BF16),
             vmem((SEQS, D), BF16),

time: 109 us -> 107 us (0.982)
  Pallas kernels: 107 us -> 105 us
    pallas_call x1, Pallas kernels: 107 us -> 105 us  [layer(): pl.pallas_call(kernel, out_shape=jax.ShapeDtypeStruct((SEQS, D), BF16), i...]
where the time goes in v3:
time: 107 us
  Pallas kernels  105 us (98%)
  local copies, waits for them, and re-layouts  1.77 us (2%)
    pallas_call x1, Pallas kernels, layer(): pl.pallas_call(kernel, out_shape=jax.ShapeDtypeStruct((SEQS, D), BF16), i...  105 us

profile of v3, /device:TPU:0, one launch (start us, length us, event | category | flops | bytes accessed | tf_op | source)
XLA Modules:
  0.0 106.9 jit_solution(4227190349850180001)
XLA Ops:
  0.0 105.2 %shard_map.109 = bf16[64,3072]{1,0:T(8,128)(2,1)} custom-call(bf16[64,3072]{1,0:T(8,128)(2,1)} %x_hbm.1, bf16[64,8192,128]{2,1,0:T(8,128)(2,1)} %bitcast.k_hbm, bf16[64,8192,128]{2,1,0:T(8,128)(2,1)} %bitcast.1.v_hbm, bf16[3072]{0:T(1024)(128)(2,1)} %ga_hbm.1, bf16[3072,768]{1,0:T(8,128)(2,1)} %wq_hbm.1, bf16[768,3072]{1,0:T(8,128)(2,1)} %wo_hbm.1, ...), custom_call_target="tpu_custom_call" | custom-call | tf_op jit(solution)/shard_map/pallas_call | solution.py:307
  105.2 1.8 %copy.13 = bf16[64,3072]{1,0:T(8,128)(2,1)} copy(bf16[64,3072]{1,0:T(8,128)(2,1)} %shard_map.109) | data formatting | bytes 786432

commit v4 on v3

--- a/solution.py
+++ b/solution.py
@@ -182,10 +182,9 @@
 
     for c in (*small, *wq_copies):
         c.start()
-    for t in range(RING):
+    for t in range(1):
         k_copy(jnp.int32(t)).start()
         v_copy(jnp.int32(t)).start()
-    loop(2 * BLOCKS, lambda i: wo_copy(i).start())
 
     barrier = pltpu.get_barrier_semaphore()
     for d in (partner, across):
@@ -196,6 +195,10 @@
     a = normed(x[...], ga[...])
     for c in wq_copies:
         c.wait()
+    for t in range(1, RING):
+        k_copy(jnp.int32(t)).start()
+        v_copy(jnp.int32(t)).start()
+    loop(2 * BLOCKS, lambda i: wo_copy(i).start())
     projected = jnp.concatenate([dot(a, wg[2]), dot(a, wg[3, :, 0:256])], 1).astype(BF16).astype(F32)
     cos, sin = turn[0:1, :], turn[1:2, :]
     for i in range(HEADS):

time: 107 us -> 106 us (level)
    pallas_call x1, Pallas kernels: 105 us -> 104 us  [layer(): pl.pallas_call(kernel, out_shape=jax.ShapeDtypeStruct((SEQS, D), BF16), i...]
where the time goes in v4:
time: 106 us
  Pallas kernels  104 us (98%)
  local copies, waits for them, and re-layouts  1.77 us (2%)
    pallas_call x1, Pallas kernels, layer(): pl.pallas_call(kernel, out_shape=jax.ShapeDtypeStruct((SEQS, D), BF16), i...  104 us

profile of v4, /device:TPU:0, one launch (start us, length us, event | category | flops | bytes accessed | tf_op | source)
XLA Modules:
  0.0 105.8 jit_solution(10701128541747217636)
XLA Ops:
  0.0 104.1 %shard_map.109 = bf16[64,3072]{1,0:T(8,128)(2,1)} custom-call(bf16[64,3072]{1,0:T(8,128)(2,1)} %x_hbm.1, bf16[64,8192,128]{2,1,0:T(8,128)(2,1)} %bitcast.k_hbm, bf16[64,8192,128]{2,1,0:T(8,128)(2,1)} %bitcast.1.v_hbm, bf16[3072]{0:T(1024)(128)(2,1)} %ga_hbm.1, bf16[3072,768]{1,0:T(8,128)(2,1)} %wq_hbm.1, bf16[768,3072]{1,0:T(8,128)(2,1)} %wo_hbm.1, ...), custom_call_target="tpu_custom_call" | custom-call | tf_op jit(solution)/shard_map/pallas_call | solution.py:310
  104.1 1.8 %copy.13 = bf16[64,3072]{1,0:T(8,128)(2,1)} copy(bf16[64,3072]{1,0:T(8,128)(2,1)} %shard_map.109) | data formatting | bytes 786432

commit v5 on v4

--- a/solution.py
+++ b/solution.py
@@ -243,11 +243,11 @@
         @pl.when(t == SEQS - RING)
         def _():
             def both(i):
-                wg_copy(i).start()
-                wu_copy(i).start()
+                wg_copy(i).start(priority=1)
+                wu_copy(i).start(priority=1)
 
             loop(FF_BLOCKS, both)
-            loop(2 * BLOCKS, lambda i: wd_copy(i).start())
+            loop(2 * BLOCKS, lambda i: wd_copy(i).start(priority=1))
 
         @pl.when(t == EARLY)
         def _():

time: 106 us -> 106 us (level)
  no operation moved by 1% of the time
where the time goes in v5:
time: 106 us
  Pallas kernels  104 us (98%)
  local copies, waits for them, and re-layouts  1.77 us (2%)
    pallas_call x1, Pallas kernels, layer(): pl.pallas_call(kernel, out_shape=jax.ShapeDtypeStruct((SEQS, D), BF16), i...  104 us

profile of v5, /device:TPU:0, one launch (start us, length us, event | category | flops | bytes accessed | tf_op | source)
XLA Modules:
  0.0 105.8 jit_solution(1481777438167946919)
XLA Ops:
  0.0 104.1 %shard_map.109 = bf16[64,3072]{1,0:T(8,128)(2,1)} custom-call(bf16[64,3072]{1,0:T(8,128)(2,1)} %x_hbm.1, bf16[64,8192,128]{2,1,0:T(8,128)(2,1)} %bitcast.k_hbm, bf16[64,8192,128]{2,1,0:T(8,128)(2,1)} %bitcast.1.v_hbm, bf16[3072]{0:T(1024)(128)(2,1)} %ga_hbm.1, bf16[3072,768]{1,0:T(8,128)(2,1)} %wq_hbm.1, bf16[768,3072]{1,0:T(8,128)(2,1)} %wo_hbm.1, ...), custom_call_target="tpu_custom_call" | custom-call | tf_op jit(solution)/shard_map/pallas_call | solution.py:310
  104.1 1.8 %copy.13 = bf16[64,3072]{1,0:T(8,128)(2,1)} copy(bf16[64,3072]{1,0:T(8,128)(2,1)} %shard_map.109) | data formatting | bytes 786432
